TPU v7x, 32 devices: a whole 2x2x4 slice. The times are simulated.
32 devices in a mesh: tm: 8 (over z, core), rows: 4 (over y, x).
Axes of the slice: x: 2, y: 2, z: 4, core: 2. Of those that a mesh axis runs over, the one named last changes fastest.
Arguments:
- frames_in: bfloat16 [16, 16, 120, 128], P('tm', 'rows'), may hold values from -25 to 25, as said below
- norm_gain: float32 [128], replicated, may hold values from 0.25 to 1.75
- norm_bias: float32 [128], replicated, may hold values from -0.5 to 0.5
- conv_weight: bfloat16 [3, 3, 3, 128, 128], replicated, may hold values from -0.109375 to 0.109375
- cotangent: bfloat16 [16, 16, 120, 128], P('tm', 'rows'), may hold values from -6 to 6
Outputs:
- output_frames: bfloat16 [16, 16, 120, 128], P('tm', 'rows')
- input_grad: bfloat16 [16, 16, 120, 128], P('tm', 'rows')
- weight_grad: float32 [128, 3456], P('rows')
- gain_grad: float32 [128], replicated
- bias_grad: float32 [128], replicated
Inputs may be any that keep to these rules, and one draw needn't show every extreme that they name: Entries of frames_in lie within 25 in magnitude.
All inputs are finite; a program needn't handle non-finite values.
Results may differ from a plain program's by a relative error of at most 0.0042.
Values may be sent and summed in bfloat16 or wider, within the bound.
A program may use at most 64 MiB of HBM per device.

v0:
```python
import math

import jax
import jax.numpy as jnp
from jax import lax
from jax.sharding import PartitionSpec as P

G = 32


EPSILON = 1e-06


def from_behind(block, axis, distance):
    devices = range(lax.axis_size(axis))
    route = [(i - distance, i) for i in devices if i - distance in devices]
    return lax.ppermute(block, axis, route)


def padded_2(block, sides, width):
    for axis, dim in sides:
        count = lax.axis_size(axis)
        forward = [(i, i + 1) for i in range(count - 1)]
        backward = [(target, source) for source, target in forward]
        low = lax.ppermute(
            lax.slice_in_dim(block, block.shape[dim] - width, None, axis=dim), axis, forward
        )
        high = lax.ppermute(lax.slice_in_dim(block, 0, width, axis=dim), axis, backward)
        block = jnp.concatenate([low, block, high], axis=dim)
    return block


def group_expand(per_channel, groups):
    channels = per_channel.shape[0]
    return jnp.repeat(
        per_channel.reshape(groups, channels // groups).sum(axis=1), channels // groups
    )


def per_device(frames_in, norm_gain, norm_bias, conv_weight, cotangent):
    frames, band_rows, columns, channels = frames_in.shape
    groups = G
    all_pixels = frames * lax.axis_size("tm") * band_rows * lax.axis_size("rows") * columns
    total_cells = all_pixels * (channels // groups)
    values = frames_in.astype(jnp.float32)
    cached = from_behind(frames_in, "tm", 1)
    stacked = jnp.concatenate([cached, frames_in], axis=0)
    margin_in = padded_2(stacked, (("rows", 1),), 1)
    channel_sum = jnp.sum(values, axis=(0, 1, 2))
    channel_sq = jnp.sum(values * values, axis=(0, 1, 2))
    group_sum = channel_sum.reshape(groups, channels // groups).sum(axis=1)
    group_sq = channel_sq.reshape(groups, channels // groups).sum(axis=1)
    group_sum, group_sq = lax.psum((group_sum, group_sq), ("tm", "rows"))
    group_mean = jnp.repeat(group_sum, channels // groups) / total_cells
    variance = jnp.repeat(group_sq, channels // groups) / total_cells - group_mean * group_mean
    inverse_std = lax.rsqrt(variance + EPSILON)
    normed = (values - group_mean) * inverse_std
    preact = normed * norm_gain + norm_bias
    margin_vals = (margin_in.astype(jnp.float32) - group_mean) * inverse_std * norm_gain + norm_bias
    margin_act = jax.nn.silu(margin_vals)
    time_keep = (jnp.arange(frames + 2) >= 2) | (lax.axis_index("tm") > 0)
    row_index = jnp.arange(band_rows + 2)
    row_keep = ((row_index >= 1) | (lax.axis_index("rows") > 0)) & (
        (row_index <= band_rows) | (lax.axis_index("rows") < lax.axis_size("rows") - 1)
    )
    keep_mask = time_keep[:, None] & row_keep[None, :]
    padded = jnp.where(keep_mask[:, :, None, None], margin_act, 0.0).astype(jnp.bfloat16)
    padded = jnp.pad(padded, ((0, 0), (0, 0), (1, 1), (0, 0)))
    pixels = frames * band_rows * columns
    conv_sum = jnp.zeros((pixels, channels), jnp.float32)
    for time_off in range(3):
        for row_off in range(3):
            for col_off in range(3):
                window = padded[
                    time_off : time_off + frames,
                    row_off : row_off + band_rows,
                    col_off : col_off + columns,
                ].reshape(pixels, channels)
                conv_sum = conv_sum + jnp.dot(
                    window,
                    conv_weight[time_off, row_off, col_off],
                    preferred_element_type=jnp.float32,
                )
    output_frames = (values + conv_sum.reshape(values.shape)).astype(jnp.bfloat16)
    grad_next = from_behind(cotangent, "tm", -1)
    grad_stack = jnp.concatenate([cotangent, grad_next], axis=0)
    grad_padded = padded_2(grad_stack, (("rows", 1),), 1)
    grad_padded = jnp.pad(grad_padded, ((0, 0), (0, 0), (1, 1), (0, 0)))
    grad_act = jnp.zeros((pixels, channels), jnp.float32)
    for time_off in range(3):
        for row_off in range(3):
            for col_off in range(3):
                grad_window = grad_padded[
                    time_off : time_off + frames,
                    row_off : row_off + band_rows,
                    col_off : col_off + columns,
                ].reshape(pixels, channels)
                flipped = conv_weight[2 - time_off, 2 - row_off, 2 - col_off].T
                grad_act = grad_act + jnp.dot(
                    grad_window, flipped, preferred_element_type=jnp.float32
                )
    grad_flat = cotangent.reshape(pixels, channels)
    pieces = []
    for time_off in range(3):
        for row_off in range(3):
            for col_off in range(3):
                window = padded[
                    time_off : time_off + frames,
                    row_off : row_off + band_rows,
                    col_off : col_off + columns,
                ].reshape(pixels, channels)
                pieces.append(
                    lax.dot_general(
                        grad_flat,
                        window,
                        (((0,), (0,)), ((), ())),
                        preferred_element_type=jnp.float32,
                    )
                )
    summed_time = lax.psum(jnp.concatenate(pieces, axis=1), "tm")
    weight_sum = lax.psum_scatter(summed_time, "rows", scatter_dimension=0, tiled=True)
    weight_grad = weight_sum * (1.0 / math.sqrt(all_pixels))
    sigmoid_v = jax.nn.sigmoid(preact)
    grad_pre = grad_act.reshape(values.shape) * sigmoid_v * (1.0 + preact * (1.0 - sigmoid_v))
    gain_part = jnp.sum(grad_pre * normed, axis=(0, 1, 2))
    bias_part = jnp.sum(grad_pre, axis=(0, 1, 2))
    gain_grad, bias_grad = lax.psum((gain_part, bias_part), ("tm", "rows"))
    mean_dn = group_expand(norm_gain * bias_grad, groups) / total_cells
    mean_dnn = group_expand(norm_gain * gain_grad, groups) / total_cells
    input_grad = inverse_std * (
        grad_pre * norm_gain - mean_dn - normed * mean_dnn
    ) + cotangent.astype(jnp.float32)
    return (output_frames, input_grad.astype(jnp.bfloat16), weight_grad, gain_grad, bias_grad)


def solution(mesh):
    placed = (P("tm", "rows", None, None), P(), P(), P(), P("tm", "rows", None, None))
    return jax.shard_map(
        per_device,
        mesh=mesh,
        in_specs=placed,
        out_specs=(
            P("tm", "rows", None, None),
            P("tm", "rows", None, None),
            P("rows", None),
            P(),
            P(),
        ),
        check_vma=False,
    )
```

profile of v0, /device:TPU:0, one launch (start us, length us, event | category | flops | bytes accessed | tf_op | source)
XLA Modules:
  0.0 223.4 jit_solution(7753915320677433358)
XLA Ops:
  7.2 2.4 %collective-permute-start = (bf16[2,4,120,128]{3,2,1,0:T(8,128)(2,1)}, bf16[2,4,120,128]{3,2,1,0:T(8,128)(2,1)S(1)}, u32[]{:S(2)}, u32[]{:S(2)}) collective-permute-start(bf16[2,4,120,128]{3,2,1,0:T(8,128)(2,1)} %param.5), channel_id=1, source_target_pairs={{0,4},{4,8},{8,12},{12,16},{16,20},{20,24},{24,28},{1,5},{5,9},{9,... | collective-permute-start | bytes 737288 | tf_op jit(solution)/shard_map/ppermute | solution.py:17
  9.7 1.3 collective-permute-start.3
  11.0 1.1 convert_reduce_fusion
  12.0 1.0 constant_dynamic-update-slice_fusion.3
  13.5 43.9 %all-reduce.3 = (f32[32]{0:T(128)S(1)}, f32[32]{0:T(128)S(1)}) all-reduce(f32[32]{0:T(128)S(1)} %reduce_sum.75, f32[32]{0:T(128)S(1)} %reduce_sum.73), channel_id=1, replica_groups=mesh['tm'=8,'rows'=4] {'tm','rows'}, use_global_device_ids=true, to_apply=%region_5.0 | all-reduce | flops 64 | bytes 512 | tf_op jit(solution)/shard_map/psum | solution.py:53
  57.8 1.0 constant_dynamic-update-slice_fusion
  58.9 4.2 %collective-permute-start.1 = (bf16[4,1,120,128]{3,2,1,0:T(8,128)(2,1)S(1)}, bf16[4,1,120,128]{3,2,1,0:T(8,128)(2,1)S(1)}, u32[]{:S(2)}, u32[]{:S(2)}) collective-permute-start(bf16[4,1,120,128]{3,2,1,0:T(8,128)(2,1)S(1)} %get-tuple-element.86), channel_id=1, source_target_pairs={{0,1},{1,2},{2,3},{4,5},{5,6},{6,7},{8,9},{9,10},{10,11},{12,13},{... | collective-permute-start | bytes 368648 | tf_op jit(solution)/shard_map/ppermute | solution.py:25
  63.1 1.3 collective-permute-start.2
  64.5 4.6 %collective-permute-start.4 = (bf16[4,1,120,128]{3,2,1,0:T(8,128)(2,1)S(1)}, bf16[4,1,120,128]{3,2,1,0:T(8,128)(2,1)S(1)}, u32[]{:S(2)}, u32[]{:S(2)}) collective-permute-start(bf16[4,1,120,128]{3,2,1,0:T(8,128)(2,1)S(1)} %get-tuple-element.84), channel_id=1, source_target_pairs={{0,1},{1,2},{2,3},{4,5},{5,6},{6,7},{8,9},{9,10},{10,11},{12,13},{... | collective-permute-start | bytes 368648 | tf_op jit(solution)/shard_map/ppermute | solution.py:25
  69.0 1.3 collective-permute-start.5
  70.4 0.6 select_convert_fusion
  71.0 0.3 fusion.31
  71.3 1.1 fusion.213
  72.4 1.6 pad_slice_fusion.8
  74.0 1.6 pad_slice_fusion.9
  75.6 0.3 fusion.13
  75.9 0.3 fusion.30
  76.2 0.3 fusion.29
  76.5 0.3 fusion.12
  76.8 0.3 fusion.28
  77.1 0.3 fusion.27
  77.3 0.3 fusion.11
  77.6 0.3 fusion.26
  77.9 0.3 fusion.25
  78.2 0.3 fusion.10
  78.5 0.3 fusion.24
  78.7 0.3 fusion.23
  79.0 0.3 fusion.9
  79.3 0.3 fusion.22
  79.6 0.3 fusion.21
  79.9 0.3 fusion.8
  80.2 0.3 fusion.20
  80.4 0.3 fusion.19
  80.7 0.3 fusion.7
  81.0 0.3 fusion.18
  81.3 0.3 fusion.17
  81.6 0.3 fusion.6
  81.9 0.3 fusion.16
  82.1 0.3 fusion.15
  82.4 0.3 fusion.5
  82.7 0.3 fusion.14
  83.0 2.0 copy.40
  85.2 0.6 copy-done.32
  85.9 0.3 fusion.36
  86.2 0.6 fusion.212
  86.7 0.6 copy-done.2
  91.6 0.2 fusion.1
  93.2 0.5 copy-done.15
  94.5 0.4 copy-done.1
  94.9 0.3 fusion.210
  95.2 41.8 %all-reduce.2 = (f32[128]{0:T(128)S(1)}, f32[128]{0:T(128)S(1)}) all-reduce(f32[128]{0:T(128)S(1)} %get-tuple-element.21, f32[128]{0:T(128)S(1)} %get-tuple-element.20), channel_id=1, replica_groups=mesh['tm'=8,'rows'=4] {'tm','rows'}, use_global_device_ids=true, to_apply=%region_10.11 | all-reduce | flops 256 | bytes 2048 | tf_op jit(solution)/shard_map/psum | solution.py:127
  138.6 0.3 copy-done.25
  139.6 0.3 copy-done.22
  140.6 0.3 copy-done.19
  141.6 0.3 copy-done.18
  142.6 0.3 copy-done.11
  143.6 0.3 copy-done.8
  144.6 0.3 copy-done.5
  145.6 0.3 copy-done.17
  146.3 2.8 %copy.41 = f32[32,3456]{0,1:T(8,128)} copy(f32[32,3456]{1,0:T(8,128)} %reduce-scatter.4.cloned.1.call-done) | data formatting | bytes 884736
  149.2 1.0 fusion.55
  150.2 63.5 %all-reduce.6.cloned.1.call-done = f32[32,3456]{0,1:T(8,128)} async-done(((f32[32,3456]{0,1:T(8,128)}), f32[32,3456]{0,1:T(8,128)}) %all-reduce.6.cloned.1.call-update) | async-done | bytes 442384 | tf_op jit(solution)/shard_map/psum | solution.py:120
  213.7 1.6 broadcast_multiply_fusion
  215.3 1.3 copy.12
  (157 shorter events, 14.3 us)
Async XLA Ops:
  7.2 63.2 %copy-start.34 = (f32[128]{0:T(128)S(1)}, f32[128]{0:T(128)}, u32[]{:S(2)}) copy-start(f32[128]{0:T(128)} %param.6) | copy-start | bytes 1540
  7.2 63.2 %copy-start.35 = (f32[128]{0:T(128)S(1)}, f32[128]{0:T(128)}, u32[]{:S(2)}) copy-start(f32[128]{0:T(128)} %param.7) | copy-start | bytes 1540
  7.2 139.1 %reduce-scatter.4.cloned.1.call-start = ((), (), s32[]{:S(2)}) async-start(), calls=%async_computation.2 | async-start | bytes 2211840
  7.2 50.6 %collective-permute-start = (bf16[2,4,120,128]{3,2,1,0:T(8,128)(2,1)}, bf16[2,4,120,128]{3,2,1,0:T(8,128)(2,1)S(1)}, u32[]{:S(2)}, u32[]{:S(2)}) collective-permute-start(bf16[2,4,120,128]{3,2,1,0:T(8,128)(2,1)} %param.5), channel_id=1, source_target_pairs={{0,4},{4,8},{8,12},{12,16},{16,20},{20,24},{24,28},{1,5},{5,9},{9,... | collective-permute-start | bytes 737288 | tf_op jit(solution)/shard_map/ppermute | solution.py:17
  9.7 54.7 %collective-permute-start.3 = (bf16[2,4,120,128]{3,2,1,0:T(8,128)(2,1)}, bf16[2,4,120,128]{3,2,1,0:T(8,128)(2,1)S(1)}, u32[]{:S(2)}, u32[]{:S(2)}) collective-permute-start(bf16[2,4,120,128]{3,2,1,0:T(8,128)(2,1)} %param.9), channel_id=1, source_target_pairs={{4,0},{8,4},{12,8},{16,12},{20,16},{24,20},{28,24},{5,1},{9,5},{13... | collective-permute-start | bytes 737288 | tf_op jit(solution)/shard_map/ppermute | solution.py:17
  57.8 13.2 %copy-start = (bf16[2,4,120,128]{3,2,1,0:T(8,128)(2,1)S(1)}, bf16[2,4,120,128]{3,2,1,0:T(8,128)(2,1)}, u32[]{:S(2)}) copy-start(bf16[2,4,120,128]{3,2,1,0:T(8,128)(2,1)} %param.9) | copy-start | bytes 737284
  58.9 11.5 %collective-permute-start.1 = (bf16[4,1,120,128]{3,2,1,0:T(8,128)(2,1)S(1)}, bf16[4,1,120,128]{3,2,1,0:T(8,128)(2,1)S(1)}, u32[]{:S(2)}, u32[]{:S(2)}) collective-permute-start(bf16[4,1,120,128]{3,2,1,0:T(8,128)(2,1)S(1)} %get-tuple-element.86), channel_id=1, source_target_pairs={{0,1},{1,2},{2,3},{4,5},{5,6},{6,7},{8,9},{9,10},{10,11},{12,13},{... | collective-permute-start | bytes 368648 | tf_op jit(solution)/shard_map/ppermute | solution.py:25
  63.1 7.3 %collective-permute-start.2 = (bf16[4,1,120,128]{3,2,1,0:T(8,128)(2,1)S(1)}, bf16[4,1,120,128]{3,2,1,0:T(8,128)(2,1)S(1)}, u32[]{:S(2)}, u32[]{:S(2)}) collective-permute-start(bf16[4,1,120,128]{3,2,1,0:T(8,128)(2,1)S(1)} %get-tuple-element.87), channel_id=1, source_target_pairs={{1,0},{2,1},{3,2},{5,4},{6,5},{7,6},{9,8},{10,9},{11,10},{13,12},{... | collective-permute-start | bytes 368648 | tf_op jit(solution)/shard_map/ppermute | solution.py:28
  64.4 8.0 %copy-start.14 = (bf16[2,4,120,128]{3,2,1,0:T(8,128)(2,1)}, bf16[2,4,120,128]{3,2,1,0:T(8,128)(2,1)S(1)}, u32[]{:S(2)}) copy-start(bf16[2,4,120,128]{3,2,1,0:T(8,128)(2,1)S(1)} %collective-permute-done.3) | copy-start | bytes 737284
  64.5 20.7 %collective-permute-start.4 = (bf16[4,1,120,128]{3,2,1,0:T(8,128)(2,1)S(1)}, bf16[4,1,120,128]{3,2,1,0:T(8,128)(2,1)S(1)}, u32[]{:S(2)}, u32[]{:S(2)}) collective-permute-start(bf16[4,1,120,128]{3,2,1,0:T(8,128)(2,1)S(1)} %get-tuple-element.84), channel_id=1, source_target_pairs={{0,1},{1,2},{2,3},{4,5},{5,6},{6,7},{8,9},{9,10},{10,11},{12,13},{... | collective-permute-start | bytes 368648 | tf_op jit(solution)/shard_map/ppermute | solution.py:25
  69.0 16.2 %collective-permute-start.5 = (bf16[4,1,120,128]{3,2,1,0:T(8,128)(2,1)S(1)}, bf16[4,1,120,128]{3,2,1,0:T(8,128)(2,1)S(1)}, u32[]{:S(2)}, u32[]{:S(2)}) collective-permute-start(bf16[4,1,120,128]{3,2,1,0:T(8,128)(2,1)S(1)} %get-tuple-element.85), channel_id=1, source_target_pairs={{1,0},{2,1},{3,2},{5,4},{6,5},{7,6},{9,8},{10,9},{11,10},{13,12},{... | collective-permute-start | bytes 368648 | tf_op jit(solution)/shard_map/ppermute | solution.py:28
  85.0 128.7 %all-reduce.6.cloned.1.call-start = ((), (), s32[]{:S(2)}) async-start(), calls=%async_computation.1 | async-start | bytes 3538944 | tf_op jit(solution)/shard_map/psum | solution.py:120
  85.2 0.7 copy-start.32
  86.1 1.2 copy-start.2
  86.1 1.2 copy-start.31
  87.6 1.1 copy-start.33
  92.7 1.0 copy-start.15
  94.0 0.9 copy-start.1
  94.2 43.7 %copy-start.28 = (bf16[2,4,120,128]{3,2,1,0:T(8,128)(2,1)S(1)}, bf16[2,4,120,128]{3,2,1,0:T(8,128)(2,1)}, u32[]{:S(2)}) copy-start(bf16[2,4,120,128]{3,2,1,0:T(8,128)(2,1)} %get-tuple-element.72) | copy-start | bytes 737284
  94.2 43.9 %copy-start.30 = (bf16[2,4,120,128]{3,2,1,0:T(8,128)(2,1)S(1)}, bf16[2,4,120,128]{3,2,1,0:T(8,128)(2,1)}, u32[]{:S(2)}) copy-start(bf16[2,4,120,128]{3,2,1,0:T(8,128)(2,1)} %get-tuple-element.48) | copy-start | bytes 737284
  94.9 43.4 %copy-start.29 = (bf16[2,4,120,128]{3,2,1,0:T(8,128)(2,1)S(1)}, bf16[2,4,120,128]{3,2,1,0:T(8,128)(2,1)}, u32[]{:S(2)}) copy-start(bf16[2,4,120,128]{3,2,1,0:T(8,128)(2,1)} %get-tuple-element.49) | copy-start | bytes 737284
  137.0 1.5 copy-start.36
  137.0 1.5 copy-start.37
  137.9 0.9 copy-start.25
  138.1 1.0 copy-start.27
  138.3 1.0 copy-start.26
  138.8 1.0 copy-start.22
  139.1 1.0 copy-start.24
  139.3 1.0 copy-start.23
  139.8 1.0 copy-start.19
  140.1 1.0 copy-start.21
  140.3 1.0 copy-start.20
  140.8 1.0 copy-start.18
  141.1 1.0 copy-start.13
  141.3 1.0 copy-start.12
  141.8 1.0 copy-start.11
  142.1 1.0 copy-start.10
  142.4 1.0 copy-start.9
  142.8 1.0 copy-start.8
  143.1 1.0 copy-start.7
  143.4 1.0 copy-start.6
  143.8 1.0 copy-start.5
  144.1 1.0 copy-start.4
  144.4 1.0 copy-start.3
  144.8 1.0 copy-start.17
  145.1 1.0 copy-start.16
Sparse Core Ops, SparseCore 0:
  85.1 34.9 reduce-scatter.3
  149.3 64.3 all-reduce.5
where the time goes:
time: 224 us; the launch traced here: 223 us
  blocking collectives  85.7 us (38%)
  waiting for transfers between devices  63.6 us (28%)
  local copies, waits for them, and re-layouts  19.3 us (9%)
  matrix products  18.9 us (8%)
  starting transfers between devices  15.3 us (7%)
  between operations  15.1 us (7%)
  other arithmetic  5.57 us (2%)
    psum x1, waiting for transfers between devices, per_device(): summed_time = lax.psum(jnp.concatenate(pieces, axis=1), 'tm')  63.5 us
    psum x1, blocking collectives, per_device(): group_sum, group_sq = lax.psum((group_sum, group_sq), ('tm', 'rows'))  43.9 us
    psum x1, blocking collectives, per_device(): gain_grad, bias_grad = lax.psum((gain_part, bias_part), ('tm', 'rows'))  41.8 us
    unnamed x81, local copies, waits for them, and re-layouts  12.2 us
    ppermute x2, starting transfers between devices, padded_2(): lax.ppermute(lax.slice_in_dim(block, block.shape[dim] - width, None, axis...  8.74 us
    dot_general x27, matrix products, per_device(): lax.dot_general(grad_flat, window, (((0,), (0,)), ((), ())), preferred_el...  7.42 us
    dot_general x27, matrix products, per_device(): jnp.dot(grad_window, flipped, preferred_element_type=jnp.float32)  5.99 us
    dot_general x27, matrix products, per_device(): jnp.dot(window, conv_weight[time_off, row_off, col_off], preferred_elemen...  5.48 us
  transfers between devices with their start and end apart: 8, of which 1 were waited for; matrix products, arithmetic and copies ran while one was open for 15% of the time, Pallas kernels for 0%

commit v1 on v0

v1 whole, which is shorter than its diff:
```python
import functools
import math

import jax
import jax.numpy as jnp
from jax import lax
from jax.experimental import pallas as pl
from jax.experimental.pallas import tpu as pltpu
from jax.sharding import PartitionSpec as P

G = 32
EPSILON = 1e-06
MESH = pl.DeviceIdType.MESH
F32, BF16 = jnp.float32, jnp.bfloat16
LANES = 128


def sigmoid(v):
    return 1.0 / (1.0 + jnp.exp(-v))


def group_total(x, width):
    lanes = x.shape[-1]
    lane = lax.broadcasted_iota(jnp.int32, x.shape, len(x.shape) - 1)
    shift = 1
    while shift < width:
        up = pltpu.roll(x, lanes - shift, axis=len(x.shape) - 1)
        down = pltpu.roll(x, shift, axis=len(x.shape) - 1)
        x = x + jnp.where((lane & shift) == 0, up, down)
        shift *= 2
    return x


def kernel(
    dims,
    x_ref, gain_ref, bias_ref, w_ref, g_ref,
    out_ref, ingrad_ref, wgrad_ref, ggain_ref, gbias_ref,
    fext, cext, x3, g3, gt, gact, gpre,
    wf, wb, arecv, bsend, brecv, csend, crecv, fin,
    st_r, st_t, gb_r, gb_t,
    halo_send, halo_recv, st_send, st_recv, gb_send, gb_recv,
    a_send, a_recv, b_send, b_recv, c_send, c_recv, d_send, d_recv,
):
    n_tm, n_rows, o_per, piece = dims
    n_z = n_tm // 2
    half = n_z * piece
    frames, band, cols, channels = x_ref.shape
    wide = x3.shape[2]
    width = channels // G
    pixels = frames * n_tm * band * n_rows * cols
    cells = pixels * width
    tm, r = lax.axis_index("tm"), lax.axis_index("rows")
    core, z = lax.rem(tm, 2), lax.div(tm, 2)

    fext[0:2] = jnp.zeros((2, band + 2, cols, channels), BF16)
    fext[2:4, 0:1] = jnp.zeros((2, 1, cols, channels), BF16)
    fext[2:4, band + 1 : band + 2] = jnp.zeros((2, 1, cols, channels), BF16)
    cext[2:4] = jnp.zeros((2, band + 2, cols, channels), BF16)
    cext[0:2, 0:1] = jnp.zeros((2, 1, cols, channels), BF16)
    cext[0:2, band + 1 : band + 2] = jnp.zeros((2, 1, cols, channels), BF16)

    def there(dt, dr):
        ok = None
        for ind, delta, n in ((tm, dt, n_tm), (r, dr, n_rows)):
            if delta:
                this = (ind + delta >= 0) & (ind + delta < n)
                ok = this if ok is None else ok & this
        return ok

    barrier = pltpu.get_barrier_semaphore()
    for d in range(1, n_rows):
        pl.semaphore_signal(barrier, inc=1, device_id=(tm, lax.rem(r + d, n_rows)), device_id_type=MESH)
    for d in range(1, n_tm):
        pl.semaphore_signal(barrier, inc=1, device_id=(lax.rem(tm + d, n_tm), r), device_id_type=MESH)
    greeted = n_rows - 1 + n_tm - 1
    for dt in (-1, 1):
        for dr in (-1, 1):
            ok = there(dt, dr)
            greeted = greeted + jnp.where(ok, 1, 0)

            @pl.when(ok)
            def _():
                pl.semaphore_signal(barrier, inc=1, device_id=(tm + dt, r + dr), device_id_type=MESH)

    def stat_step(p, carry):
        s, q = carry
        v = x_ref[lax.div(p, band), lax.rem(p, band)].astype(F32)
        v = v.reshape(cols // 8, 8, channels)
        return s + jnp.sum(v, axis=0), q + jnp.sum(v * v, axis=0)

    zero8 = jnp.zeros((8, channels), F32)
    s8, q8 = lax.fori_loop(0, frames * band, stat_step, (zero8, zero8))
    row8 = lax.broadcasted_iota(jnp.int32, (8, channels), 0)

    def two_rows(first, second):
        a = jnp.sum(first, axis=0, keepdims=True)
        b = jnp.sum(second, axis=0, keepdims=True)
        return jnp.where(row8 == 0, a, jnp.where(row8 == 1, b, 0.0))

    st_r[r] = two_rows(s8, q8)
    pl.semaphore_wait(barrier, greeted)

    def remote(src, dst, ssem, rsem, dev):
        return pltpu.make_async_remote_copy(
            src_ref=src, dst_ref=dst, send_sem=ssem, recv_sem=rsem, device_id=dev, device_id_type=MESH
        )

    def rows_copies(buf, ssem, rsem, incoming):
        made = []
        for d in range(1, n_rows):
            slot = lax.rem(r + n_rows - d, n_rows) if incoming else r
            made.append(remote(buf.at[slot], buf.at[slot], ssem.at[d - 1], rsem.at[d - 1], (tm, lax.rem(r + d, n_rows))))
        return made

    def tm_copies(buf, ssem, rsem, incoming):
        made = []
        for d in range(1, n_tm):
            slot = lax.rem(tm + n_tm - d, n_tm) if incoming else tm
            k = n_rows - 2 + d
            made.append(remote(buf.at[slot], buf.at[slot], ssem.at[k], rsem.at[k], (lax.rem(tm + d, n_tm), r)))
        return made

    def start_all(copies):
        for copy in copies:
            copy.start()

    def wait_recv(copies):
        for copy in copies:
            copy.wait_recv()

    def wait_send(copies):
        for copy in copies:
            copy.wait_send()

    def slot_sum(buf, n):
        total = buf[0]
        for j in range(1, n):
            total = total + buf[j]
        return total

    start_all(rows_copies(st_r, st_send, st_recv, False))

    last = slice(band - 1, band)
    first = slice(0, 1)
    body = slice(1, band + 1)
    top, bottom = slice(0, 1), slice(band + 1, band + 2)
    every = slice(None)
    halos = [
        (g_ref, cext, (0, 1), last, slice(0, 2), top),
        (g_ref, cext, (0, -1), first, slice(0, 2), bottom),
        (g_ref, cext, (-1, 1), last, slice(2, 4), top),
        (g_ref, cext, (-1, -1), first, slice(2, 4), bottom),
        (g_ref, cext, (-1, 0), every, slice(2, 4), body),
        (x_ref, fext, (0, 1), last, slice(2, 4), top),
        (x_ref, fext, (0, -1), first, slice(2, 4), bottom),
        (x_ref, fext, (1, 1), last, slice(0, 2), top),
        (x_ref, fext, (1, -1), first, slice(0, 2), bottom),
        (x_ref, fext, (1, 0), every, slice(0, 2), body),
    ]

    def halo_copy(k):
        src, dst, (dt, dr), rows_from, frames_to, rows_to = halos[k]
        return remote(
            src.at[:, rows_from], dst.at[frames_to, rows_to], halo_send.at[k], halo_recv.at[k], (tm + dt, r + dr)
        )

    for k in range(len(halos)):
        dt, dr = halos[k][2]

        @pl.when(there(dt, dr))
        def _(k=k):
            halo_copy(k).start()

    def halo_wait_recv(ks):
        for k in ks:
            dt, dr = halos[k][2]

            @pl.when(there(-dt, -dr))
            def _(k=k):
                halo_copy(k).wait_recv()

    pad_rows = jnp.zeros((wide - cols, channels), F32)

    def three_shifts(dst, f, h, v):
        v = jnp.concatenate([v, pad_rows], axis=0)
        dst[f, h, :, 0:channels] = pltpu.roll(v, 1, axis=0).astype(BF16)
        dst[f, h, :, channels : 2 * channels] = v.astype(BF16)
        dst[f, h, :, 2 * channels : 3 * channels] = pltpu.roll(v, wide - 1, axis=0).astype(BF16)

    def own_cot(p, carry):
        f, h = lax.div(p, band), lax.rem(p, band)
        three_shifts(g3, f, h + 1, g_ref[f, h].astype(F32))
        return carry

    lax.fori_loop(0, frames * band, own_cot, 0)
    own = g3[0:frames, 1 : band + 1, :, channels : 2 * channels].reshape(frames * band * wide, channels)
    gt[...] = own.T

    wait_recv(rows_copies(st_r, st_send, st_recv, True))
    st_t[tm] = slot_sum(st_r, n_rows)
    start_all(tm_copies(st_t, st_send, st_recv, False))

    halo_wait_recv(range(0, 5))

    def edge_cot(p, carry):
        f, h = lax.div(p, 2), lax.rem(p, 2) * (band + 1)
        three_shifts(g3, f, h, cext[f, h].astype(F32))
        return carry

    lax.fori_loop(0, 2 * frames, edge_cot, 0)

    def next_cot(p, carry):
        f, h = lax.div(p, band + 2) + frames, lax.rem(p, band + 2)
        three_shifts(g3, f, h, cext[f, h].astype(F32))
        return carry

    lax.fori_loop(0, frames * (band + 2), next_cot, 0)

    plane = band * wide
    for t in range(frames):
        acc = jnp.zeros((plane, channels), F32)
        for a in range(3):
            for b in range(3):
                rhs = jnp.concatenate([w_ref[2 - a, 2 - b, 2 - c] for c in range(3)], axis=1)
                acc = acc + lax.dot_general(
                    g3[t + a, b : b + band].reshape(plane, 3 * channels),
                    rhs,
                    (((1,), (1,)), ((), ())),
                    preferred_element_type=F32,
                )
        gact[t] = acc.reshape(band, wide, channels)

    wait_recv(tm_copies(st_t, st_send, st_recv, True))
    stats = group_total(slot_sum(st_t, n_tm), width) / cells
    mean = stats[0:1]
    inverse_std = lax.rsqrt(stats[1:2] - mean * mean + EPSILON)
    gain, bias = gain_ref[...], bias_ref[...]

    halo_wait_recv(range(5, 10))

    def act_rows(f, h, v, keep):
        preact = (v.astype(F32) - mean) * inverse_std * gain + bias
        three_shifts(x3, f, h, preact * sigmoid(preact) * keep)

    def own_act(p, carry):
        f, h = lax.div(p, band), lax.rem(p, band)
        act_rows(f + 2, h + 1, x_ref[f, h], 1.0)
        return carry

    lax.fori_loop(0, frames * band, own_act, 0)

    def keep_of(f, h):
        dead = ((f < 2) & (tm == 0)) | ((h == 0) & (r == 0)) | ((h == band + 1) & (r == n_rows - 1))
        return jnp.where(dead, 0.0, 1.0)

    def edge_act(p, carry):
        f, h = lax.div(p, 2) + 2, lax.rem(p, 2) * (band + 1)
        act_rows(f, h, fext[f, h], keep_of(f, h))
        return carry

    lax.fori_loop(0, 2 * frames, edge_act, 0)

    def cached_act(p, carry):
        f, h = lax.div(p, band + 2), lax.rem(p, band + 2)
        act_rows(f, h, fext[f, h], keep_of(f, h))
        return carry

    lax.fori_loop(0, 2 * (band + 2), cached_act, 0)

    rows_used = 27 * o_per
    if rows_used < 2 * half:
        wf[:, rows_used:] = jnp.zeros((n_rows, 2 * half - rows_used, channels), F32)
        wb[:, rows_used:] = jnp.zeros((n_rows, 2 * half - rows_used, channels), BF16)
    for a in range(3):
        for b in range(3):
            res = jnp.dot(
                gt[...],
                x3[a : a + frames, b : b + band].reshape(frames * plane, 3 * channels),
                preferred_element_type=F32,
            )
            for c in range(3):
                at = (9 * a + 3 * b + c) * o_per
                tile = res[:, c * channels : (c + 1) * channels].reshape(n_rows, o_per, channels)
                wf[:, at : at + o_per] = tile
                wb[:, at : at + o_per] = tile.astype(BF16)

    mine = pl.ds(pl.multiple_of(core * half, 16), half)
    other = pl.ds(pl.multiple_of((1 - core) * half, 16), half)
    stage_a = remote(wb.at[:, other], arecv, a_send, a_recv, (tm + 1 - 2 * core, r))
    stage_a.start()

    def forward(t):
        acc = jnp.zeros((plane, channels), F32)
        for a in range(3):
            for b in range(3):
                acc = acc + jnp.dot(
                    x3[t + a, b : b + band].reshape(plane, 3 * channels),
                    w_ref[a, b].reshape(3 * channels, channels),
                    preferred_element_type=F32,
                )
        acc = acc.reshape(band, wide, channels)[:, :cols]
        out_ref[t] = (x_ref[t].astype(F32) + acc).astype(BF16)

    forward(0)

    stage_a.wait_recv()
    summed = wf[:, mine] + arecv[...].astype(F32)
    wf[:, mine] = summed
    bsend[...] = summed.astype(BF16)
    stage_b = []
    for d in range(1, n_rows):
        to = lax.rem(r + d, n_rows)
        stage_b.append(remote(bsend.at[to], brecv.at[d - 1], b_send.at[d - 1], b_recv.at[d - 1], (tm, to)))
    start_all(stage_b)

    def pre_step(p, carry):
        s, q = carry
        t, h = lax.div(p, band), lax.rem(p, band)
        normed = (x_ref[t, h].astype(F32) - mean) * inverse_std
        preact = normed * gain + bias
        sig = sigmoid(preact)
        gp = gact[t, h, 0:cols] * sig * (1.0 + preact * (1.0 - sig))
        gpre[t, h] = gp
        prod = (gp * normed).reshape(cols // 8, 8, channels)
        return s + jnp.sum(prod, axis=0), q + jnp.sum(gp.reshape(cols // 8, 8, channels), axis=0)

    s8, q8 = lax.fori_loop(0, frames * band, pre_step, (zero8, zero8))
    gb_r[r] = two_rows(s8, q8)
    start_all(rows_copies(gb_r, gb_send, gb_recv, False))

    for t in range(1, frames):
        forward(t)

    wait_recv(rows_copies(gb_r, gb_send, gb_recv, True))
    gb_t[tm] = slot_sum(gb_r, n_rows)
    start_all(tm_copies(gb_t, gb_send, gb_recv, False))

    wait_recv(stage_b)
    total = wf[r, mine]
    for d in range(1, n_rows):
        total = total + brecv[d - 1].astype(F32)
    wf[r, mine] = total
    csend[...] = total.astype(BF16)
    stage_c = []
    for d in range(1, n_z):
        to = lax.rem(z + d, n_z)
        chunk = pl.ds(pl.multiple_of(to * piece, 16), piece)
        stage_c.append(
            remote(csend.at[chunk], crecv.at[d - 1], c_send.at[d - 1], c_recv.at[d - 1], (2 * to + core, r))
        )
    start_all(stage_c)

    wait_recv(tm_copies(gb_t, gb_send, gb_recv, True))
    both = slot_sum(gb_t, n_tm)
    ggain_ref[...] = both[0:1]
    gbias_ref[...] = both[1:2]
    means = group_total(both * gain, width) / cells
    mean_dnn, mean_dn = means[0:1], means[1:2]

    wait_recv(stage_c)
    total = wf[r, pl.ds(pl.multiple_of(core * half + z * piece, 16), piece)]
    for d in range(1, n_z):
        total = total + crecv[d - 1].astype(F32)
    spot = pl.ds(pl.multiple_of(core * half + z * piece, 16), piece)
    fin[spot] = (total * (1.0 / math.sqrt(pixels))).astype(BF16)
    stage_d, stage_d_in = [], []
    for d in range(1, n_tm):
        to, frm = lax.rem(tm + d, n_tm), lax.rem(tm + n_tm - d, n_tm)
        theirs = pl.ds(pl.multiple_of(lax.rem(frm, 2) * half + lax.div(frm, 2) * piece, 16), piece)
        stage_d.append(remote(fin.at[spot], fin.at[spot], d_send.at[d - 1], d_recv.at[d - 1], (to, r)))
        stage_d_in.append(remote(fin.at[theirs], fin.at[theirs], d_send.at[d - 1], d_recv.at[d - 1], (to, r)))
    start_all(stage_d)

    def final_step(p, carry):
        t, h = lax.div(p, band), lax.rem(p, band)
        normed = (x_ref[t, h].astype(F32) - mean) * inverse_std
        grad = inverse_std * (gpre[t, h] * gain - mean_dn - normed * mean_dnn) + g_ref[t, h].astype(F32)
        ingrad_ref[t, h] = grad.astype(BF16)
        return carry

    lax.fori_loop(0, frames * band, final_step, 0)

    wait_recv(stage_d_in)
    for tap in range(27):
        wgrad_ref[:, tap * channels : (tap + 1) * channels] = fin[tap * o_per : (tap + 1) * o_per].astype(F32)

    for k in range(len(halos)):
        dt, dr = halos[k][2]

        @pl.when(there(dt, dr))
        def _(k=k):
            halo_copy(k).wait_send()

    wait_send(rows_copies(st_r, st_send, st_recv, False))
    wait_send(tm_copies(st_t, st_send, st_recv, False))
    wait_send(rows_copies(gb_r, gb_send, gb_recv, False))
    wait_send(tm_copies(gb_t, gb_send, gb_recv, False))
    stage_a.wait_send()
    wait_send(stage_b)
    wait_send(stage_c)
    wait_send(stage_d)


def per_device(frames_in, norm_gain, norm_bias, conv_weight, cotangent):
    frames, band, cols, channels = frames_in.shape
    n_tm, n_rows = lax.axis_size("tm"), lax.axis_size("rows")
    wide = -(-(cols + 1) // 16) * 16
    o_per = channels // n_rows
    n_z = n_tm // 2
    piece = -(-27 * o_per // (n_tm * 16)) * 16
    half = n_z * piece
    small = n_rows - 1 + n_tm - 1
    dma = pltpu.SemaphoreType.DMA
    vmem = pl.BlockSpec(memory_space=pltpu.VMEM)
    outs = pl.pallas_call(
        functools.partial(kernel, (n_tm, n_rows, o_per, piece)),
        out_shape=(
            jax.ShapeDtypeStruct(frames_in.shape, BF16),
            jax.ShapeDtypeStruct(frames_in.shape, BF16),
            jax.ShapeDtypeStruct((o_per, 27 * channels), F32),
            jax.ShapeDtypeStruct((1, channels), F32),
            jax.ShapeDtypeStruct((1, channels), F32),
        ),
        in_specs=[vmem] * 5,
        out_specs=(vmem,) * 5,
        scratch_shapes=[
            pltpu.VMEM((frames + 2, band + 2, cols, channels), BF16),
            pltpu.VMEM((frames + 2, band + 2, cols, channels), BF16),
            pltpu.VMEM((frames + 2, band + 2, wide, 3 * channels), BF16),
            pltpu.VMEM((frames + 2, band + 2, wide, 3 * channels), BF16),
            pltpu.VMEM((channels, frames * band * wide), BF16),
            pltpu.VMEM((frames, band, wide, channels), F32),
            pltpu.VMEM((frames, band, cols, channels), F32),
            pltpu.VMEM((n_rows, 2 * half, channels), F32),
            pltpu.VMEM((n_rows, 2 * half, channels), BF16),
            pltpu.VMEM((n_rows, half, channels), BF16),
            pltpu.VMEM((n_rows, half, channels), BF16),
            pltpu.VMEM((n_rows - 1, half, channels), BF16),
            pltpu.VMEM((half, channels), BF16),
            pltpu.VMEM((n_z - 1, piece, channels), BF16),
            pltpu.VMEM((2 * half, channels), BF16),
            pltpu.VMEM((n_rows, 8, channels), F32),
            pltpu.VMEM((n_tm, 8, channels), F32),
            pltpu.VMEM((n_rows, 8, channels), F32),
            pltpu.VMEM((n_tm, 8, channels), F32),
            dma((10,)), dma((10,)),
            dma((small,)), dma((small,)),
            dma((small,)), dma((small,)),
            dma, dma,
            dma((n_rows - 1,)), dma((n_rows - 1,)),
            dma((n_z - 1,)), dma((n_z - 1,)),
            dma((n_tm - 1,)), dma((n_tm - 1,)),
        ],
        compiler_params=pltpu.CompilerParams(
            collective_id=0, has_side_effects=True, vmem_limit_bytes=56 * 1024 * 1024
        ),
    )(frames_in, norm_gain.reshape(1, channels), norm_bias.reshape(1, channels), conv_weight, cotangent)
    return outs[0], outs[1], outs[2], outs[3].reshape(channels), outs[4].reshape(channels)


def solution(mesh):
    placed = (P("tm", "rows", None, None), P(), P(), P(), P("tm", "rows", None, None))
    return jax.shard_map(
        per_device,
        mesh=mesh,
        in_specs=placed,
        out_specs=(
            P("tm", "rows", None, None),
            P("tm", "rows", None, None),
            P("rows", None),
            P(),
            P(),
        ),
        check_vma=False,
    )
```

time: 224 us -> 46.8 us (0.21)
  blocking collectives: 85.7 us -> 0 us
  waiting for transfers between devices: 63.6 us -> 0 us
  Pallas kernels: 0 us -> 41.6 us
  matrix products: 18.9 us -> 0 us
  starting transfers between devices: 15.3 us -> 0 us
  local copies, waits for them, and re-layouts: 19.3 us -> 4.37 us
  between operations: 15.1 us -> 0.66 us
  other arithmetic: 5.57 us -> 0 us
    psum x2 -> x0, blocking collectives: 85.7 us -> none  [the longest x1 43.9 us: per_device(): group_sum, group_sq = lax.psum((group_sum, group_sq), ('tm', 'rows'))]
    psum x1 -> x0, waiting for transfers between devices: 63.5 us -> none  [per_device(): summed_time = lax.psum(jnp.concatenate(pieces, axis=1), 'tm')]
    pallas_call x0 -> x1, Pallas kernels: none -> 41.6 us  [per_device(): pl.pallas_call(functools.partial(kernel, (n_tm, n_rows, o_per, piece)), o...]
    dot_general x81 -> x0, matrix products: 18.9 us -> none  [the longest x27 7.42 us: per_device(): lax.dot_general(grad_flat, window, (((0,), (0,)), ((), ())), preferred_el...]
    ppermute x6 -> x0, starting transfers between devices: 15 us -> none  [the longest x2 8.74 us: padded_2(): lax.ppermute(lax.slice_in_dim(block, block.shape[dim] - width, None, axis...]
    unnamed x81 -> x13, local copies, waits for them, and re-layouts: 12.2 us -> 4.37 us
    slice x6 -> x0, local copies, waits for them, and re-layouts: 4.97 us -> none  [the longest x3 4.36 us: per_device(): padded[time_off:time_off + frames, row_off:row_off + band_rows, col_off:c...]
  transfers between devices with their start and end apart: 8 -> 0, of which waited for: 1 -> 0; matrix products, arithmetic and copies ran while one was open for 15% -> 0% of each run, Pallas kernels for 0% -> 0%
where the time goes in v1:
time: 46.8 us; the launch traced here: 46.6 us
  Pallas kernels  41.6 us (89%)
  local copies, waits for them, and re-layouts  4.37 us (9%)
  between operations  0.66 us (1%)
    pallas_call x1, Pallas kernels, per_device(): pl.pallas_call(functools.partial(kernel, (n_tm, n_rows, o_per, piece)), o...  41.6 us
    unnamed x13, local copies, waits for them, and re-layouts  4.37 us

profile of v1, /device:TPU:0, one launch (start us, length us, event | category | flops | bytes accessed | tf_op | source)
XLA Modules:
  0.0 46.6 jit_solution(10797156892585422367)
XLA Ops:
  0.6 41.6 %shard_map.92 = (bf16[2,4,120,128]{3,2,1,0:T(8,128)(2,1)}, bf16[2,4,120,128]{3,2,1,0:T(8,128)(2,1)}, f32[32,3456]{1,0:T(8,128)}, f32[1,128]{1,0:T(1,128)}, f32[1,128]{1,0:T(1,128)}) custom-call(bf16[2,4,120,128]{3,2,1,0:T(8,128)(2,1)} %x_ref.1, f32[1,128]{1,0:T(1,128)} %bitcast.4, f32[1,128]{1,0:T(1,128)} %bitcast.5, bf16[3,3,3,128,128]{4,3,2,1,0:T(8,128)(2,1)} %w_ref.1, ...), custom_call_target="tpu_custom_call" | custom-call | tf_op jit(solution)/shard_map/pallas_call | solution.py:415
  42.2 0.0 copy-start.1
  42.3 0.0 copy-start
  42.3 1.7 %copy.15 = bf16[2,4,120,128]{3,2,1,0:T(8,128)(2,1)} copy(bf16[2,4,120,128]{3,2,1,0:T(8,128)(2,1)} %get-tuple-element.20) | data formatting | bytes 491520
  44.0 0.0 copy-done.1
  44.0 0.7 %copy.16 = bf16[2,4,120,128]{3,2,1,0:T(8,128)(2,1)} copy(bf16[2,4,120,128]{3,2,1,0:T(8,128)(2,1)S(1)} %copy-done.1) | data formatting | bytes 491520
  44.7 0.0 copy-done
  44.7 0.0 copy-start.3
  44.7 0.8 %copy.17 = f32[32,3456]{1,0:T(8,128)} copy(f32[32,3456]{1,0:T(8,128)S(1)} %copy-done) | data formatting | bytes 884736
  45.4 0.0 copy-done.3
  45.4 0.0 copy-start.2
  45.5 0.5 %copy.18 = f32[128]{0:T(128)} copy(f32[128]{0:T(128)S(1)} %bitcast.7) | data formatting | bytes 1024
  46.0 0.2 copy-done.2
  46.1 0.5 %copy.19 = f32[128]{0:T(128)} copy(f32[128]{0:T(128)S(1)} %bitcast.6) | data formatting | bytes 1024
Async XLA Ops:
  42.2 1.7 %copy-start.1 = (bf16[2,4,120,128]{3,2,1,0:T(8,128)(2,1)S(1)}, bf16[2,4,120,128]{3,2,1,0:T(8,128)(2,1)}, u32[]{:S(2)}) copy-start(bf16[2,4,120,128]{3,2,1,0:T(8,128)(2,1)} %get-tuple-element.21) | copy-start | bytes 737284
  42.3 2.4 %copy-start = (f32[32,3456]{1,0:T(8,128)S(1)}, f32[32,3456]{1,0:T(8,128)}, u32[]{:S(2)}) copy-start(f32[32,3456]{1,0:T(8,128)} %get-tuple-element.22) | copy-start | bytes 1327108
  44.7 0.8 %copy-start.3 = (f32[1,128]{1,0:T(1,128)S(1)}, f32[1,128]{1,0:T(1,128)}, u32[]{:S(2)}) copy-start(f32[1,128]{1,0:T(1,128)} %get-tuple-element.13) | copy-start | bytes 1540
  45.4 0.7 %copy-start.2 = (f32[1,128]{1,0:T(1,128)S(1)}, f32[1,128]{1,0:T(1,128)}, u32[]{:S(2)}) copy-start(f32[1,128]{1,0:T(1,128)} %get-tuple-element.14) | copy-start | bytes 1540
